TPU v7x, 32 devices: a whole 2x2x4 slice. The times are simulated.
32 devices in a mesh: tm: 8 (over z, x), space: 4 (over y, core).
Axes of the slice: x: 2, y: 2, z: 4, core: 2. Of those that a mesh axis runs over, the one named last changes fastest.
Arguments:
- forcing: bfloat16 [128, 256, 256], P('tm', 'space'), may hold values from -0.59765625 to 0.59765625
- starting_heat: bfloat16 [256, 256], P('space'), may hold values from -3 to 3, as said below
Outputs:
- heat_history: float32 [128, 256, 256], P('tm', 'space')
- history: float32 [2, 32], P(None, 'tm')
- change: float32 [2, 32], P(None, 'tm')
Inputs may be any that keep to these rules, and one draw needn't show every extreme that they name: starting_heat is a combination of the 64 sine modes with both indices from 1 to 8, scaled so that its largest magnitude is 3.
All inputs are finite; a program needn't handle non-finite values.
Results may differ from a plain program's by a relative error of at most 0.0016.
Values may be sent and summed in bfloat16 or wider, within the bound.
A program may use at most 64 MiB of HBM per device.

v0:
```python
import math

import jax
import jax.numpy as jnp
from jax import lax
from jax.sharding import PartitionSpec as P

FINE_FACTOR = 4
COARSE_FACTOR = 4
ITERS = 2


DURATION = 0.004


def passed_along(block, axis, distance):
    devices = range(lax.axis_size(axis))
    route = [(i - distance, i) for i in devices if i - distance in devices]
    return lax.ppermute(block, axis, route)


def prefix_2(array, axis, combine, identity, reverse):
    devices, mine = lax.axis_size(axis), lax.axis_index(axis)
    everything = jax.tree.map(lambda part: lax.all_gather(part, axis), array)
    start = jax.tree.map(
        lambda part, zero: jnp.broadcast_to(jnp.asarray(zero, part.dtype), part.shape),
        array,
        identity,
    )

    def lap(k, before):
        at = devices - 1 - k if reverse else k
        reached = at > mine if reverse else at < mine
        new = combine(before, jax.tree.map(lambda part: part[at], everything))
        return jax.tree.map(lambda a, b: jnp.where(reached, a, b), new, before)

    return lax.fori_loop(0, devices, lap, start)


def sine_table(sample_locations, number_type):
    numbers = jnp.arange(1, sample_locations + 1, dtype=jnp.int32)
    product = numbers[:, None] * numbers[None, :] % (2 * (sample_locations + 1))
    angles = jnp.pi * product.astype(jnp.float32) / (sample_locations + 1)
    return (math.sqrt(2.0 / (sample_locations + 1)) * jnp.sin(angles)).astype(number_type)


def eigenvalues(sample_locations, first_mode, mode_count):
    numbers = (first_mode + jnp.arange(mode_count, dtype=jnp.int32) + 1).astype(jnp.float32)
    halves = jnp.sin(jnp.pi * numbers / (2 * (sample_locations + 1)))
    return 4.0 * (sample_locations + 1) ** 2 * halves * halves


def smoothing_pass(starts, sources, factor):
    current = starts
    visited = []
    for column in range(sources.shape[1] - 1):
        current = factor * current + sources[:, column]
        visited.append(current)
    return visited


def compose_powers(earlier, later):
    return (earlier[0] * later[0], later[0] * earlier[1] + later[1])


def shards(forcing, starting_heat):
    step_count, row_count, sample_locations = forcing.shape
    block_width = sample_locations // lax.axis_size("space")
    intervals = step_count // FINE_FACTOR
    blocks = intervals // COARSE_FACTOR
    steps_all = step_count * lax.axis_size("tm")
    table_half = sine_table(sample_locations, jnp.bfloat16)
    table_full = sine_table(sample_locations, jnp.float32)
    stacked = jnp.concatenate([starting_heat[None], forcing], axis=0)
    halved = jnp.dot(
        stacked.reshape(-1, sample_locations), table_half, preferred_element_type=jnp.float32
    )
    halved = halved.astype(jnp.bfloat16).reshape(step_count + 1, row_count, sample_locations)
    turned = lax.all_to_all(halved, "space", split_axis=2, concat_axis=1, tiled=True)
    spectra = jnp.einsum("xi,tiy->txy", table_half, turned, preferred_element_type=jnp.float32)
    first_mode = lax.axis_index("space") * block_width
    decay_rates = (
        eigenvalues(sample_locations, 0, sample_locations)[:, None]
        + eigenvalues(sample_locations, first_mode, block_width)[None, :]
    )
    increment_duration = DURATION / steps_all
    per_increment_factor = 1.0 / (1.0 + increment_duration * decay_rates)
    mid_gain = 1.0 / (1.0 + FINE_FACTOR * increment_duration * decay_rates)
    top_gain = 1.0 / (1.0 + FINE_FACTOR * COARSE_FACTOR * increment_duration * decay_rates)
    block_gain = top_gain
    for block_index in range(1, blocks):
        block_gain = block_gain * top_gain
    start_field = spectra[0]
    sources = (per_increment_factor * spectra[1:]).reshape(
        intervals, FINE_FACTOR, sample_locations, block_width
    )
    at_start = lax.axis_index("tm") == 0
    values = jnp.zeros((intervals, sample_locations, block_width), jnp.float32)
    pinned_boundary = jnp.where(at_start, start_field, jnp.zeros_like(start_field))
    history_rows = []
    change_rows = []
    for iteration in range(ITERS):
        ends_rest = smoothing_pass(values[:-1], sources[1:], per_increment_factor)[-1]
        relaxed_rest = per_increment_factor * ends_rest + sources[1:, -1]
        arrived = passed_along(relaxed_rest[-1], "tm", 1)
        ends_first = smoothing_pass(pinned_boundary[None], sources[:1], per_increment_factor)[-1]
        relaxed = jnp.concatenate(
            [per_increment_factor * ends_first + sources[:1, -1], relaxed_rest], 0
        )
        arrived = jnp.where(at_start, start_field, arrived)
        ends_two = smoothing_pass(
            jnp.concatenate([arrived[None], relaxed[:-1]], 0), sources, per_increment_factor
        )[-1]
        residual = sources[:, -1] + per_increment_factor * ends_two - relaxed
        local_norms = jnp.sum(residual * residual, axis=(1, 2))
        coarse_rhs = residual.reshape(blocks, COARSE_FACTOR, sample_locations, block_width)
        running = coarse_rhs[:, 0]
        for column in range(1, COARSE_FACTOR):
            running = mid_gain * running + coarse_rhs[:, column]
        local_end = running[0]
        for block_index in range(1, blocks):
            local_end = top_gain * local_end + running[block_index]
        prefix = prefix_2(
            (block_gain, local_end),
            "tm",
            compose_powers,
            (jnp.ones_like(block_gain), jnp.zeros_like(local_end)),
            False,
        )
        incoming_value = prefix[1]
        coarse_list = []
        current = incoming_value
        for block_index in range(blocks):
            current = top_gain * current + running[block_index]
            coarse_list.append(current)
        coarse_values = jnp.stack(coarse_list)
        begins = jnp.concatenate([incoming_value[None], coarse_values[:-1]], 0)
        pieces = smoothing_pass(begins, coarse_rhs, mid_gain)
        correction = jnp.stack(pieces + [coarse_values], axis=1).reshape(
            intervals, sample_locations, block_width
        )
        values = relaxed + correction
        corr_sq = jnp.sum(correction * correction, axis=(1, 2))
        value_sq = jnp.sum(values * values, axis=(1, 2))
        norm_total, corr_total, value_total = lax.psum((local_norms, corr_sq, value_sq), "space")
        history_rows.append(jnp.sqrt(norm_total / (sample_locations * sample_locations)))
        change_rows.append(jnp.sqrt(corr_total / value_total))
        pinned_boundary = arrived + incoming_value
    starts = jnp.concatenate([pinned_boundary[None], values[:-1]], 0)
    inside = smoothing_pass(starts, sources, per_increment_factor)
    spectral_path = jnp.stack(inside + [values], axis=1).reshape(
        step_count, sample_locations, block_width
    )
    rows_back = jnp.einsum(
        "xi,tiy->txy", table_full, spectral_path, precision=lax.Precision.HIGHEST
    ).astype(jnp.bfloat16)
    returned = lax.all_to_all(rows_back, "space", split_axis=1, concat_axis=2, tiled=True)
    physical_rows = jnp.dot(
        returned.reshape(-1, sample_locations), table_half, preferred_element_type=jnp.float32
    )
    heat_history = physical_rows.reshape(step_count, row_count, sample_locations)
    history = jnp.stack(history_rows)
    change = jnp.stack(change_rows)
    return (heat_history, history, change)


def solution(mesh):
    return jax.shard_map(
        shards,
        mesh=mesh,
        in_specs=(P("tm", "space", None), P("space", None)),
        out_specs=(P("tm", "space", None), P(None, "tm"), P(None, "tm")),
        check_vma=False,
    )
```

profile of v0, /device:TPU:27, one launch (start us, length us, event | category | flops | bytes accessed | tf_op | source)
XLA Modules:
  0.0 182.2 jit_solution(14928108210097297900)
XLA Ops:
  0.6 1.1 pad_maximum_fusion.1
  1.7 1.4 convolution_convert_fusion
  3.1 1.0 copy.50
  4.1 1.6 reshape.775
  5.7 4.1 %all-to-all-start = ((bf16[4,2,34816]{2,1,0:T(2,128)(2,1)}), bf16[4,2,34816]{2,1,0:T(2,128)(2,1)S(1)}, u32[]{:S(2)}, u32[]{:S(2)}) async-start(bf16[4,2,34816]{2,1,0:T(2,128)(2,1)} %reshape.775), calls=%async_computation | async-start | bytes 1114112 | tf_op jit(solution)/shard_map/all_to_all | solution.py:79
  10.0 8.0 %all-to-all-done = bf16[4,2,34816]{2,1,0:T(2,128)(2,1)S(1)} async-done(((bf16[4,2,34816]{2,1,0:T(2,128)(2,1)}), bf16[4,2,34816]{2,1,0:T(2,128)(2,1)S(1)}, u32[]{:S(2)}, u32[]{:S(2)}) %all-to-all-start) | async-done | bytes 557088 | tf_op jit(solution)/shard_map/all_to_all | solution.py:79
  18.0 1.2 reshape.776
  19.2 0.9 copy.87
  20.1 0.7 all_to_all.27
  20.8 1.4 convolution_bitcast_fusion
  22.5 0.1 bitcast_add_fusion.27
  22.6 1.3 collective-permute-start
  23.9 0.7 fusion.51
  24.6 3.0 %collective-permute-done = f32[256,64]{0,1:T(8,128)S(1)} collective-permute-done((f32[256,64]{0,1:T(8,128)S(1)}, f32[256,64]{0,1:T(8,128)S(1)}, u32[]{:S(2)}, u32[]{:S(2)}) %collective-permute-start) | collective-permute-done | bytes 65568 | tf_op jit(solution)/shard_map/ppermute | solution.py:19
  27.6 0.1 fusion.14
  27.8 0.1 bitcast_add_fusion.24
  27.9 0.4 copy-done.7
  28.3 0.2 copy-done.5
  28.5 27.7 %all_gather.12 = f32[8,256,64]{1,2,0:T(8,128)} all-gather(f32[1,256,64]{1,2,0:T(8,128)S(1)} %get-tuple-element.307), channel_id=1, replica_groups=mesh['tm'=8,'space'=4] {'tm'}, dimensions={0}, use_global_device_ids=true | all-gather | bytes 589824 | tf_op jit(solution)/shard_map/all_gather | solution.py:24
  56.2 1.4 copy.60
  57.6 27.0 %all_gather.13 = f32[8,256,64]{1,2,0:T(8,128)} all-gather(f32[1,256,64]{1,2,0:T(8,128)S(1)} %get-tuple-element.306), channel_id=1, replica_groups=mesh['tm'=8,'space'=4] {'tm'}, dimensions={0}, use_global_device_ids=true | all-gather | bytes 589824 | tf_op jit(solution)/shard_map/all_gather | solution.py:24
  84.6 8.3 %while.28 = (s32[]{:T(128)}, f32[256,64]{1,0:T(8,128)S(1)}, s32[]{:T(128)}, f32[8,256,64]{2,1,0:T(8,128)S(1)}, f32[8,256,64]{1,2,0:T(8,128)}, /*index=5*/s32[]{:T(128)}, s32[]{:T(128)}) while((s32[]{:T(128)}, f32[256,64]{1,0:T(8,128)S(1)}, s32[]{:T(128)}, f32[8,256,64]{2,1,0:T(8,128)S(1)}, f32[8,256,64]{1,2,0:T(8,128)}, ...), condition=%wide.region_1.2_spmd.clone, body=%wide.region_0.1_spmd.clone.sunk | while | flops 65540 | bytes 524393 | solution.py:37
  84.6 0.8 constant_dynamic-slice_fusion.4
  85.6 0.8 constant_dynamic-slice_fusion.4
  86.6 0.8 constant_dynamic-slice_fusion.4
  87.7 0.8 constant_dynamic-slice_fusion.4
  88.7 0.8 constant_dynamic-slice_fusion.4
  89.7 0.8 constant_dynamic-slice_fusion.4
  90.8 0.8 constant_dynamic-slice_fusion.4
  91.8 0.8 constant_dynamic-slice_fusion.4
  92.9 1.2 fusion.105
  94.2 0.7 multiply_reduce_fusion.1
  94.9 1.3 collective-permute-start.1
  96.3 3.7 %collective-permute-done.1 = f32[256,64]{0,1:T(8,128)S(1)} collective-permute-done((f32[256,64]{0,1:T(8,128)S(1)}, f32[256,64]{0,1:T(8,128)S(1)}, u32[]{:S(2)}, u32[]{:S(2)}) %collective-permute-start.1) | collective-permute-done | bytes 65568 | tf_op jit(solution)/shard_map/ppermute | solution.py:19
  99.9 0.8 bitcast_select_fusion
  100.8 0.1 fusion.22
  101.0 26.8 %all_gather.14 = f32[8,256,64]{1,2,0:T(8,128)} all-gather(f32[1,256,64]{1,2,0:T(8,128)S(1)} %bitcast_add_fusion.11), channel_id=1, replica_groups=mesh['tm'=8,'space'=4] {'tm'}, dimensions={0}, use_global_device_ids=true | all-gather | bytes 589824 | tf_op jit(solution)/shard_map/all_gather | solution.py:24
  127.8 8.3 %while.29 = (s32[]{:T(128)}, f32[256,64]{1,0:T(8,128)S(1)}, s32[]{:T(128)}, f32[8,256,64]{2,1,0:T(8,128)S(1)}, f32[8,256,64]{1,2,0:T(8,128)}, /*index=5*/s32[]{:T(128)}, s32[]{:T(128)}) while((s32[]{:T(128)}, f32[256,64]{1,0:T(8,128)S(1)}, s32[]{:T(128)}, f32[8,256,64]{2,1,0:T(8,128)S(1)}, f32[8,256,64]{1,2,0:T(8,128)}, ...), condition=%wide.region_3.4_spmd.clone, body=%wide.region_2.3_spmd.clone.sunk | while | flops 65540 | bytes 524393 | solution.py:37
  127.8 0.9 constant_dynamic-slice_fusion.5
  128.9 0.8 constant_dynamic-slice_fusion.5
  129.9 0.8 constant_dynamic-slice_fusion.5
  131.0 0.8 constant_dynamic-slice_fusion.5
  132.0 0.8 constant_dynamic-slice_fusion.5
  133.1 0.8 constant_dynamic-slice_fusion.5
  134.1 0.8 constant_dynamic-slice_fusion.5
  135.1 0.8 constant_dynamic-slice_fusion.5
  136.2 0.1 fusion.106
  136.4 0.7 multiply_reduce_fusion
  137.1 0.1 bitcast_add_fusion.2
  137.2 0.1 pad_maximum_fusion
  137.3 0.1 copy.72
  137.4 2.1 %fusion.2 = bf16[16,256,64]{1,2,0:T(8,128)(2,1)S(1)} fusion(f32[16,256,64]{1,2,0:T(8,128)S(1)} %bitcast.390, s32[256]{0:T(256)S(1)} %iota_add_fusion), kind=kOutput, calls=%fused_computation.11 | convolution fusion | flops 806223872 | bytes 1573888 | tf_op jit(solution)/shard_map/xi,tiy->txy/dot_general | solution.py:154
  139.5 1.0 copy.73
  140.4 1.6 reshape.777
  142.0 25.3 %all-to-all-start.1 = ((bf16[4,2,32768]{2,1,0:T(2,128)(2,1)}), bf16[4,2,32768]{2,1,0:T(2,128)(2,1)S(1)}, u32[]{:S(2)}, u32[]{:S(2)}) async-start(bf16[4,2,32768]{2,1,0:T(2,128)(2,1)} %reshape.777), calls=%async_computation.1 | async-start | bytes 1048576 | tf_op jit(solution)/shard_map/all_to_all | solution.py:157
  167.3 0.3 fusion.47
  167.6 0.3 copy-done.10
  167.9 8.6 %all-reduce = (f32[4]{0:T(128)S(1)}, f32[4]{0:T(128)S(1)}, f32[4]{0:T(128)S(1)}, f32[4]{0:T(128)S(1)}, f32[4]{0:T(128)S(1)}, /*index=5*/f32[4]{0:T(128)S(1)}) all-reduce(f32[4]{0:T(128)S(1)} %get-tuple-element.260, f32[4]{0:T(128)S(1)} %get-tuple-element.259, f32[4]{0:T(128)S(1)} %copy-done.11, ...), channel_id=1, replica_groups=mesh['tm'=8,'space'=4] {'space'}, use_global_device_ids=true, to_apply=%region_7.8 | all-reduce | flops 24 | bytes 192 | tf_op jit(solution)/shard_map/psum | solution.py:145
  176.5 0.6 pad_maximum_fusion.6
  177.1 0.6 pad_maximum_fusion.5
  177.7 0.7 reshape.778
  178.4 0.8 copy.88
  179.3 0.7 dot_general.17
  179.9 2.3 %fusion.61 = f32[16,64,256]{2,1,0:T(8,128)} fusion(bf16[16,64,256]{2,1,0:T(8,128)(2,1)S(1)} %dot_general.17, s32[256]{0:T(256)S(1)} %iota_add_fusion), kind=kOutput, calls=%fused_computation.105 | convolution fusion | flops 134938624 | bytes 1573888 | tf_op jit(solution)/shard_map/dot_general | solution.py:158
  (77 shorter events, 3.5 us)
Async XLA Ops:
  5.7 12.3 %all-to-all-start = ((bf16[4,2,34816]{2,1,0:T(2,128)(2,1)}), bf16[4,2,34816]{2,1,0:T(2,128)(2,1)S(1)}, u32[]{:S(2)}, u32[]{:S(2)}) async-start(bf16[4,2,34816]{2,1,0:T(2,128)(2,1)} %reshape.775), calls=%async_computation | async-start | bytes 1114112 | tf_op jit(solution)/shard_map/all_to_all | solution.py:79
  22.2 5.4 %copy-start = (f32[17,256,64]{1,2,0:T(8,128)}, f32[17,256,64]{1,2,0:T(8,128)S(1)}, u32[]{:S(2)}) copy-start(f32[17,256,64]{1,2,0:T(8,128)S(1)} %convolution_bitcast_fusion) | copy-start | bytes 3342340
  22.4 2.2 %copy-start.6 = (f32[1,4,256,64]{2,3,1,0:T(8,128)}, f32[1,4,256,64]{2,3,1,0:T(8,128)S(1)}, u32[]{:S(2)}) copy-start(f32[1,4,256,64]{2,3,1,0:T(8,128)S(1)} %slice_bitcast_fusion) | copy-start | bytes 786436
  22.6 5.0 %collective-permute-start = (f32[256,64]{0,1:T(8,128)S(1)}, f32[256,64]{0,1:T(8,128)S(1)}, u32[]{:S(2)}, u32[]{:S(2)}) collective-permute-start(f32[256,64]{0,1:T(8,128)S(1)} %slice_bitcast_fusion.7), channel_id=1, source_target_pairs={{0,4},{4,8},{8,12},{12,16},{16,20},{20,24},{24,28},{1,5},{5,9},{9,... | collective-permute-start | bytes 196616 | tf_op jit(solution)/shard_map/ppermute | solution.py:19
  27.6 0.6 copy-start.7
  27.8 0.7 copy-start.5
  56.2 28.4 %copy-start.2 = (f32[256,64]{1,0:T(8,128)S(1)}, f32[256,64]{1,0:T(8,128)}, u32[]{:S(2)}) copy-start(f32[256,64]{1,0:T(8,128)} %custom-call) | copy-start | bytes 196612
  94.2 6.6 %copy-start.3 = (f32[256,64]{0,1:T(8,128)}, f32[256,64]{0,1:T(8,128)S(1)}, u32[]{:S(2)}) copy-start(f32[256,64]{0,1:T(8,128)S(1)} %get-tuple-element.304) | copy-start | bytes 196612
  94.9 5.0 %collective-permute-start.1 = (f32[256,64]{0,1:T(8,128)S(1)}, f32[256,64]{0,1:T(8,128)S(1)}, u32[]{:S(2)}, u32[]{:S(2)}) collective-permute-start(f32[256,64]{0,1:T(8,128)S(1)} %slice_bitcast_fusion.6), channel_id=1, source_target_pairs={{0,4},{4,8},{8,12},{12,16},{16,20},{20,24},{24,28},{1,5},{5,9},{9,... | collective-permute-start | bytes 196616 | tf_op jit(solution)/shard_map/ppermute | solution.py:19
  100.8 27.0 %copy-start.1 = (f32[256,64]{1,0:T(8,128)S(1)}, f32[256,64]{1,0:T(8,128)}, u32[]{:S(2)}) copy-start(f32[256,64]{1,0:T(8,128)} %custom-call.1) | copy-start | bytes 196612
  127.8 8.5 %copy-start.4 = (f32[256,64]{0,1:T(8,128)S(1)}, f32[256,64]{0,1:T(8,128)}, u32[]{:S(2)}) copy-start(f32[256,64]{0,1:T(8,128)} %copy-done.3) | copy-start | bytes 196612
  140.4 26.9 %copy-start.8 = (f32[256,64]{0,1:T(8,128)S(1)}, f32[256,64]{0,1:T(8,128)}, u32[]{:S(2)}) copy-start(f32[256,64]{0,1:T(8,128)} %copy-done.7) | copy-start | bytes 196612
  140.4 26.9 %copy-start.9 = (f32[3,256,64]{1,2,0:T(8,128)S(1)}, f32[3,256,64]{1,2,0:T(8,128)}, u32[]{:S(2)}) copy-start(f32[3,256,64]{1,2,0:T(8,128)} %fusion.51) | copy-start | bytes 589828
  142.0 35.7 %all-to-all-start.1 = ((bf16[4,2,32768]{2,1,0:T(2,128)(2,1)}), bf16[4,2,32768]{2,1,0:T(2,128)(2,1)S(1)}, u32[]{:S(2)}, u32[]{:S(2)}) async-start(bf16[4,2,32768]{2,1,0:T(2,128)(2,1)} %reshape.777), calls=%async_computation.1 | async-start | bytes 1048576 | tf_op jit(solution)/shard_map/all_to_all | solution.py:157
  167.3 0.7 copy-start.10
  167.3 0.7 copy-start.11
where the time goes:
time: 185 us; the launch traced here: 182 us
  blocking collectives  90.1 us (49%)
  starting transfers between devices  32 us (17%)
  local copies, waits for them, and re-layouts  27.9 us (15%)
  waiting for transfers between devices  14.7 us (8%)
  other arithmetic  9.09 us (5%)
  matrix products  7.09 us (4%)
    all_gather x3, blocking collectives, prefix_2(): everything = jax.tree.map(lambda part: lax.all_gather(part, axis), array)  81.5 us
    all_to_all x1, starting transfers between devices, shards(): lax.all_to_all(rows_back, 'space', split_axis=1, concat_axis=2, tiled=True)  25.3 us
    dynamic_slice x32, local copies, waits for them, and re-layouts, lap(): new = combine(before, jax.tree.map(lambda part: part[at], everything))  15.1 us
    psum x1, blocking collectives, shards(): lax.psum((local_norms, corr_sq, value_sq), 'space')  8.58 us
    all_to_all x1, waiting for transfers between devices, shards(): lax.all_to_all(halved, 'space', split_axis=2, concat_axis=1, tiled=True)  8.01 us
    unnamed x29, local copies, waits for them, and re-layouts  7.44 us
    ppermute x2, waiting for transfers between devices, passed_along(): return lax.ppermute(block, axis, route)  6.67 us
    all_to_all x1, starting transfers between devices, shards(): lax.all_to_all(halved, 'space', split_axis=2, concat_axis=1, tiled=True)  4.12 us
  transfers between devices with their start and end apart: 4, of which 3 were waited for; matrix products, arithmetic and copies ran while one was open for 1% of the time, Pallas kernels for 0%

commit v1 on v0

v1 whole, which is shorter than its diff:
```python
import functools
import math

import jax
import jax.numpy as jnp
import numpy as np
from jax import lax
from jax.experimental import pallas as pl
from jax.experimental.pallas import tpu as pltpu
from jax.sharding import PartitionSpec as P

FINE_FACTOR = 4
COARSE_FACTOR = 4
ITERS = 2
DURATION = 0.004
LANES = 128
MESH = pl.DeviceIdType.MESH
F32 = jnp.float32
BF16 = jnp.bfloat16


def sine_table(size):
    numbers = np.arange(1, size + 1, dtype=np.int64)
    product = numbers[:, None] * numbers[None, :] % (2 * (size + 1))
    return (math.sqrt(2.0 / (size + 1)) * np.sin(np.pi * product / (size + 1))).astype(np.float32)


def eigenvalues(size):
    numbers = np.arange(1, size + 1, dtype=np.float64)
    return 4.0 * (size + 1) ** 2 * np.sin(np.pi * numbers / (2 * (size + 1))) ** 2


def tables(size, slabs):
    width = size // slabs
    full = sine_table(size)
    half = full.astype(BF16)
    low = (full - half.astype(np.float32)).astype(BF16)
    back = np.zeros((slabs, 2, width, 2, size), BF16)
    for part in range(2):
        back[:, part, :, part, :] = half.reshape(slabs, width, size)
    back = back.reshape(2 * size, 2 * size)
    mu = eigenvalues(size)
    rate = mu.reshape(1, 2, size // 2, 1) + mu.reshape(slabs, 1, 1, width)
    rate = rate.transpose(0, 2, 1, 3).reshape(slabs, size // 2, 2 * width).astype(np.float32)
    return half, low, back, rate


def swap(low, a, b):
    half = LANES // 2
    return (
        jnp.where(low, a, pltpu.roll(b, half, 1)),
        jnp.where(low, pltpu.roll(a, half, 1), b),
    )


def kernel(n_tm, n_sp, rounds, f_ref, s_ref, half_ref, low_ref, back_ref, rate_ref,
           out_ref, hist_ref, chg_ref,
           sbuf, rbuf, src, path, tbuf, ubuf, lbuf, gbuf, zbuf, lrx, grx, zrx, vref, aref, stats, srx,
           f_send, f_recv, f_local, b_send, b_recv, b_local, t_send, t_recv, q_send, q_recv):
    tm, sp = lax.axis_index("tm"), lax.axis_index("space")
    steps, rows, size = f_ref.shape
    pairs = steps // 2
    inner = size // 2
    first = tm == 0
    distances = [1, 2] + [d for d in rounds if d > 2]
    peers = [lax.rem(sp + k, n_sp) for k in range(n_sp)]
    low = lax.broadcasted_iota(jnp.int32, (1, LANES), 1) < LANES // 2

    barrier = pltpu.get_barrier_semaphore()
    count = n_sp - 1
    for k in range(1, n_sp):
        pl.semaphore_signal(barrier, inc=1, device_id={"space": peers[k]}, device_id_type=MESH)
    for d in distances:
        @pl.when(tm + d < n_tm)
        def _():
            pl.semaphore_signal(barrier, inc=1, device_id={"tm": tm + d}, device_id_type=MESH)

        @pl.when(tm >= d)
        def _():
            pl.semaphore_signal(barrier, inc=1, device_id={"tm": tm - d}, device_id_type=MESH)
        count = count + (tm + d < n_tm).astype(jnp.int32) + (tm >= d).astype(jnp.int32)

    groups = [(p, p + 2) for p in range(0, pairs, 2)]
    groups[0] = (0, 2)
    f_groups = [(pairs, pairs + 1)] + groups

    def exchange(source, target, lo, hi, index, send, recv, local):
        copies = []
        for k in range(1, n_sp):
            copies.append(pltpu.make_async_remote_copy(
                src_ref=source.at[peers[k], pl.ds(lo, hi - lo)],
                dst_ref=target.at[sp, pl.ds(lo, hi - lo)],
                send_sem=send.at[index, k], recv_sem=recv.at[index, k],
                device_id={"space": peers[k]}, device_id_type=MESH))
        copies.append(pltpu.make_async_copy(
            source.at[sp, pl.ds(lo, hi - lo)], target.at[sp, pl.ds(lo, hi - lo)], local.at[index]))
        return copies

    forward = []
    for index, (lo, hi) in enumerate(f_groups):
        if lo == pairs:
            a = jnp.dot(s_ref[...], half_ref[...], preferred_element_type=F32)
            b = a
        else:
            a = jnp.dot(f_ref[lo:hi].reshape((hi - lo) * rows, size), half_ref[...],
                        preferred_element_type=F32)
            b = jnp.dot(f_ref[pairs + lo:pairs + hi].reshape((hi - lo) * rows, size), half_ref[...],
                        preferred_element_type=F32)
        for g in range(size // LANES):
            window = slice(g * LANES, (g + 1) * LANES)
            even, odd = swap(low, a[:, window], b[:, window])
            sbuf[2 * g, lo:hi] = even.astype(BF16).reshape(hi - lo, rows, LANES)
            sbuf[2 * g + 1, lo:hi] = odd.astype(BF16).reshape(hi - lo, rows, LANES)
        if index == 0:
            pl.semaphore_wait(barrier, count)
        copies = exchange(sbuf, rbuf, lo, hi, index, f_send, f_recv, f_local)
        for copy in copies:
            copy.start()
        forward.append(copies)

    step = DURATION / (steps * n_tm)
    rate = rate_ref[sp]
    gain = 1.0 / (1.0 + step * rate)
    mid = 1.0 / (1.0 + FINE_FACTOR * step * rate)
    top = 1.0 / (1.0 + FINE_FACTOR * COARSE_FACTOR * step * rate)
    gain4 = (gain * gain) * (gain * gain)
    mid2 = mid * mid
    push = mid2 * mid * gain4
    ratio = push / top

    begin = None
    for index, (lo, hi) in enumerate(f_groups):
        for copy in forward[index][:-1]:
            copy.wait_recv()
        forward[index][-1].wait()
        block = jnp.concatenate(
            [rbuf[:, p].reshape(size, LANES) for p in range(lo, hi)], axis=1)
        spectra = jnp.dot(half_ref[...], block, preferred_element_type=F32)
        for q, p in enumerate(range(lo, hi)):
            window = slice(q * LANES, (q + 1) * LANES)
            one, two = swap(low, spectra[:inner, window], spectra[inner:, window])
            if p == pairs:
                begin = one
                path[0] = one
            else:
                src[p] = gain * one
                src[pairs + p] = gain * two

    for i in range(COARSE_FACTOR):
        total = src[FINE_FACTOR * i]
        for j in range(1, FINE_FACTOR):
            total = gain * total + src[FINE_FACTOR * i + j]
        tbuf[i] = total
    begin = path[0]

    vref[0] = jnp.where(first, begin, 0.0)
    for i in range(1, COARSE_FACTOR + 1):
        vref[i] = jnp.zeros_like(begin)

    sent = []

    def along(source, target, slot, it, distance):
        copy = pltpu.make_async_remote_copy(
            src_ref=source, dst_ref=target,
            send_sem=t_send.at[it, slot], recv_sem=t_recv.at[it, slot],
            device_id={"tm": tm + distance}, device_id_type=MESH)
        sent.append((copy, distance))

        @pl.when(tm + distance < n_tm)
        def _():
            copy.start()
        return copy

    for it in range(ITERS):
        last = COARSE_FACTOR - 1
        newest = gain4 * vref[last] + tbuf[last]
        lbuf[it] = newest
        shift = along(lbuf.at[it], lrx.at[it], 0, it, 1)
        relaxed = [gain4 * vref[i] + tbuf[i] for i in range(last)] + [newest]
        residual = [None] + [gain4 * (relaxed[i - 1] - vref[i]) for i in range(1, COARSE_FACTOR)]
        local = residual[1]
        for i in range(2, COARSE_FACTOR):
            local = mid * local + residual[i]
        gbuf[it] = local - jnp.where(first, 0.0, push * vref[0]) + ratio * newest
        near = along(gbuf.at[it], grx.at[it, 0], 1, it, 1)
        far = along(gbuf.at[it], grx.at[it, 1], 2, it, 2)
        for i in range(COARSE_FACTOR):
            ubuf[i] = relaxed[i]
        zbuf[it, 0] = jnp.zeros_like(begin)
        aref[...] = begin

        @pl.when(tm >= 1)
        def _():
            shift.wait_recv()
            aref[...] = lrx[it]
            near.wait_recv()
            zbuf[it, 0] = grx[it, 0]

        @pl.when(tm >= 2)
        def _():
            far.wait_recv()
            zbuf[it, 0] = zbuf[it, 0] + top * grx[it, 1]
        power = top * top
        for r, d in enumerate(rounds):
            copy = along(zbuf.at[it, r], zrx.at[it, r], 3 + r, it, d)
            zbuf[it, r + 1] = zbuf[it, r]

            @pl.when(tm >= d)
            def _():
                copy.wait_recv()
                zbuf[it, r + 1] = zbuf[it, r + 1] + power * zrx[it, r]
            power = power * power
        arrived = aref[...]
        incoming = jnp.where(first, 0.0, zbuf[it, len(rounds)] - ratio * arrived)
        before = vref[0]
        keep = incoming
        for i in range(COARSE_FACTOR):
            if i == 0:
                res = gain4 * (arrived - before)
                run = res
            else:
                res = gain4 * (ubuf[i - 1] - vref_old)
                run = mid * run + res
            vref_old = vref[i + 1]
            if i < COARSE_FACTOR - 1:
                keep = mid * keep + res
            else:
                keep = top * incoming + run
            value = ubuf[i] + keep
            vref[i + 1] = value
            for kind, item in enumerate((res, keep, value)):
                at = (kind * ITERS + it) * COARSE_FACTOR + i
                stats[at:at + 1] = jnp.sum(item * item, axis=0, keepdims=True)
        vref[0] = arrived + incoming

    tallies = []
    for k in range(1, n_sp):
        copy = pltpu.make_async_remote_copy(
            src_ref=stats, dst_ref=srx.at[sp], send_sem=q_send.at[k], recv_sem=q_recv.at[k],
            device_id={"space": peers[k]}, device_id_type=MESH)
        copy.start()
        tallies.append(copy)

    for i in range(COARSE_FACTOR):
        current = vref[i]
        for j in range(FINE_FACTOR - 1):
            current = gain * current + src[FINE_FACTOR * i + j]
            path[FINE_FACTOR * i + j] = current
        path[FINE_FACTOR * i + FINE_FACTOR - 1] = vref[i + 1]

    for copies in forward:
        for copy in copies[:-1]:
            copy.wait_send()
    backward = []
    for index, (lo, hi) in enumerate(groups):
        columns = []
        for p in range(lo, hi):
            upper, lower = swap(low, path[p], path[pairs + p])
            columns.append(jnp.concatenate([upper, lower], axis=0))
        block = jnp.concatenate(columns, axis=1)
        high = block.astype(BF16)
        rest = (block - high.astype(F32)).astype(BF16)
        back = jnp.dot(low_ref[...], high, preferred_element_type=F32)
        back = back + jnp.dot(half_ref[...], rest, preferred_element_type=F32)
        back = back + jnp.dot(half_ref[...], high, preferred_element_type=F32)
        back = back.astype(BF16)
        for j in range(n_sp):
            for q, p in enumerate(range(lo, hi)):
                bsend_block = back[j * rows:(j + 1) * rows, q * LANES:(q + 1) * LANES]
                sbuf[j, pairs + 1 + p] = bsend_block
        copies = exchange(sbuf, rbuf, pairs + 1 + lo, pairs + 1 + hi, index, b_send, b_recv, b_local)
        for copy in copies:
            copy.start()
        backward.append(copies)

    for index, (lo, hi) in enumerate(groups):
        for copy in backward[index][:-1]:
            copy.wait_recv()
        backward[index][-1].wait()
        block = jnp.concatenate(
            [rbuf[j, pairs + 1 + lo:pairs + 1 + hi].reshape((hi - lo) * rows, LANES)
             for j in range(n_sp)], axis=1)
        heat = jnp.dot(block, back_ref[...], preferred_element_type=F32)
        out_ref[lo:hi] = heat[:, :size].reshape(hi - lo, rows, size)
        out_ref[pairs + lo:pairs + hi] = heat[:, size:].reshape(hi - lo, rows, size)

    total = stats[...]
    for k in range(1, n_sp):
        tallies[k - 1].wait_recv()
        total = total + srx[lax.rem(sp - k + n_sp, n_sp)]
    total = jnp.sum(total, axis=1, keepdims=True)
    points = ITERS * COARSE_FACTOR
    residual_norm = jnp.sqrt(total[:points] / (size * size))
    relative = jnp.sqrt(total[points:2 * points] / total[2 * points:3 * points])
    shape = (ITERS, COARSE_FACTOR)
    where = (lax.broadcasted_iota(jnp.int32, shape, 0) * COARSE_FACTOR
             + lax.broadcasted_iota(jnp.int32, shape, 1))
    hist = jnp.zeros(shape, F32)
    chg = jnp.zeros(shape, F32)
    for k in range(points):
        hist = jnp.where(where == k, residual_norm[k:k + 1], hist)
        chg = jnp.where(where == k, relative[k:k + 1], chg)
    hist_ref[...] = hist
    chg_ref[...] = chg

    for copies in backward:
        for copy in copies[:-1]:
            copy.wait_send()
    for copy in tallies:
        copy.wait_send()
    for copy, distance in sent:
        @pl.when(tm + distance < n_tm)
        def _():
            copy.wait_send()


def shards(forcing, starting_heat):
    steps, rows, size = forcing.shape
    n_tm, n_sp = lax.axis_size("tm"), lax.axis_size("space")
    assert steps == FINE_FACTOR * COARSE_FACTOR and 2 * rows == LANES
    pairs = steps // 2
    rounds = []
    reach = 2
    while reach < n_tm - 1:
        rounds.append(reach)
        reach *= 2
    half, low, back, rate = tables(size, n_sp)
    state = (size // 2, LANES)
    slots = len(rounds) + 1
    chunks = pairs // 2 + 1
    stat_rows = 3 * ITERS * COARSE_FACTOR
    dma = pltpu.SemaphoreType.DMA
    vmem = pl.BlockSpec(memory_space=pltpu.VMEM)
    return pl.pallas_call(
        functools.partial(kernel, n_tm, n_sp, tuple(rounds)),
        out_shape=(
            jax.ShapeDtypeStruct((steps, rows, size), F32),
            jax.ShapeDtypeStruct((ITERS, COARSE_FACTOR), F32),
            jax.ShapeDtypeStruct((ITERS, COARSE_FACTOR), F32),
        ),
        in_specs=[vmem] * 6,
        out_specs=(vmem,) * 3,
        scratch_shapes=[
            pltpu.VMEM((n_sp, 2 * pairs + 1, rows, LANES), BF16),
            pltpu.VMEM((n_sp, 2 * pairs + 1, rows, LANES), BF16),
            pltpu.VMEM((steps,) + state, F32),
            pltpu.VMEM((steps,) + state, F32),
            pltpu.VMEM((COARSE_FACTOR,) + state, F32),
            pltpu.VMEM((COARSE_FACTOR,) + state, F32),
            pltpu.VMEM((ITERS,) + state, F32),
            pltpu.VMEM((ITERS,) + state, F32),
            pltpu.VMEM((ITERS, slots) + state, F32),
            pltpu.VMEM((ITERS,) + state, F32),
            pltpu.VMEM((ITERS, 2) + state, F32),
            pltpu.VMEM((ITERS, slots) + state, F32),
            pltpu.VMEM((COARSE_FACTOR + 1,) + state, F32),
            pltpu.VMEM(state, F32),
            pltpu.VMEM((stat_rows, LANES), F32),
            pltpu.VMEM((n_sp, stat_rows, LANES), F32),
            dma((chunks, n_sp)), dma((chunks, n_sp)), dma((chunks,)),
            dma((chunks, n_sp)), dma((chunks, n_sp)), dma((chunks,)),
            dma((ITERS, 3 + len(rounds))), dma((ITERS, 3 + len(rounds))),
            dma((n_sp,)), dma((n_sp,)),
        ],
        compiler_params=pltpu.CompilerParams(collective_id=0, has_side_effects=True),
    )(forcing, starting_heat, jnp.asarray(half), jnp.asarray(low), jnp.asarray(back),
      jnp.asarray(rate))


def solution(mesh):
    return jax.shard_map(
        shards,
        mesh=mesh,
        in_specs=(P("tm", "space", None), P("space", None)),
        out_specs=(P("tm", "space", None), P(None, "tm"), P(None, "tm")),
        check_vma=False,
    )
```

time: 185 us -> 44.6 us (0.24); the launches traced: 182 us -> 44.4 us
  blocking collectives: 90.1 us -> 0 us
  Pallas kernels: 0 us -> 40.2 us
  starting transfers between devices: 32 us -> 0 us
  local copies, waits for them, and re-layouts: 27.9 us -> 3.52 us
  waiting for transfers between devices: 14.7 us -> 0 us
  other arithmetic: 9.09 us -> 0 us
  matrix products: 7.09 us -> 0 us
    all_gather x3 -> x0, blocking collectives: 81.5 us -> none  [prefix_2(): everything = jax.tree.map(lambda part: lax.all_gather(part, axis), array)]
    pallas_call x0 -> x1, Pallas kernels: none -> 40.2 us  [shards(): pl.pallas_call(functools.partial(kernel, n_tm, n_sp, tuple(rounds)), out_...]
    all_to_all x2 -> x0, starting transfers between devices: 29.4 us -> none  [the longest x1 25.3 us: shards(): lax.all_to_all(rows_back, 'space', split_axis=1, concat_axis=2, tiled=True)]
    dynamic_slice x32 -> x0, local copies, waits for them, and re-layouts: 15.1 us -> none  [lap(): new = combine(before, jax.tree.map(lambda part: part[at], everything))]
    psum x1 -> x0, blocking collectives: 8.58 us -> none  [shards(): lax.psum((local_norms, corr_sq, value_sq), 'space')]
    all_to_all x2 -> x0, waiting for transfers between devices: 8.01 us -> none  [the longest x1 8.01 us: shards(): lax.all_to_all(halved, 'space', split_axis=2, concat_axis=1, tiled=True)]
    dot_general x4 -> x0, matrix products: 7.09 us -> none  [the longest x1 2.32 us: shards(): jnp.dot(returned.reshape(-1, sample_locations), table_half, preferred_ele...]
    ppermute x2 -> x0, waiting for transfers between devices: 6.67 us -> none  [passed_along(): return lax.ppermute(block, axis, route)]
  transfers between devices with their start and end apart: 4 -> 0, of which waited for: 3 -> 0; matrix products, arithmetic and copies ran while one was open for 1% -> 0% of each run, Pallas kernels for 0% -> 0%
where the time goes in v1:
time: 44.6 us; the launch traced here: 44.4 us
  Pallas kernels  40.2 us (90%)
  local copies, waits for them, and re-layouts  3.52 us (8%)
  between operations  0.65 us (1%)
    pallas_call x1, Pallas kernels, shards(): pl.pallas_call(functools.partial(kernel, n_tm, n_sp, tuple(rounds)), out_...  40.2 us
    unnamed x7, local copies, waits for them, and re-layouts  3.52 us

profile of v1, /device:TPU:27, one launch (start us, length us, event | category | flops | bytes accessed | tf_op | source)
XLA Modules:
  0.0 44.4 jit_solution(17154038373684552400)
XLA Ops:
  0.6 40.2 %shard_map.85 = (f32[16,64,256]{2,1,0:T(8,128)}, f32[2,4]{1,0:T(2,128)}, f32[2,4]{1,0:T(2,128)}) custom-call(bf16[16,64,256]{2,1,0:T(8,128)(2,1)} %f_ref.1, bf16[64,256]{1,0:T(8,128)(2,1)} %s_ref.1, bf16[256,256]{1,0:T(8,128)(2,1)} %constant.8.clone.half_ref, bf16[256,256]{1,0:T(8,128)(2,1)} %constant.9.clone.low_ref, ...), custom_call_target="tpu_custom_call" | custom-call | tf_op jit(solution)/shard_map/pallas_call | solution.py:334
  40.9 0.0 copy-start.1
  40.9 2.3 %copy.12 = f32[16,64,256]{2,1,0:T(8,128)} copy(f32[16,64,256]{2,1,0:T(8,128)} %get-tuple-element.6) | data formatting | bytes 2097152
  43.2 0.0 copy-done.1
  43.2 0.0 copy-start
  43.2 0.6 %copy.13 = f32[2,4]{1,0:T(2,128)} copy(f32[2,4]{1,0:T(2,128)S(1)} %copy-done.1) | data formatting | bytes 64
  43.7 0.1 copy-done
  43.8 0.6 %copy.14 = f32[2,4]{1,0:T(2,128)} copy(f32[2,4]{1,0:T(2,128)S(1)} %copy-done) | data formatting | bytes 64
Async XLA Ops:
  40.9 2.3 %copy-start.1 = (f32[2,4]{1,0:T(2,128)S(1)}, f32[2,4]{1,0:T(2,128)}, u32[]{:S(2)}) copy-start(f32[2,4]{1,0:T(2,128)} %get-tuple-element.7) | copy-start | bytes 100
  43.2 0.7 %copy-start = (f32[2,4]{1,0:T(2,128)S(1)}, f32[2,4]{1,0:T(2,128)}, u32[]{:S(2)}) copy-start(f32[2,4]{1,0:T(2,128)} %get-tuple-element.8) | copy-start | bytes 100

commit v2 on v1

--- a/solution.py
+++ b/solution.py
@@ -55,7 +55,7 @@
 
 def kernel(n_tm, n_sp, rounds, f_ref, s_ref, half_ref, low_ref, back_ref, rate_ref,
            out_ref, hist_ref, chg_ref,
-           sbuf, rbuf, src, path, tbuf, ubuf, lbuf, gbuf, zbuf, lrx, grx, zrx, vref, aref, stats, srx,
+           sbuf, rbuf, src, path, tbuf, ubuf, gbuf, zbuf, lrx, wrx, grx, zrx, vref, aref, stats, srx,
            f_send, f_recv, f_local, b_send, b_recv, b_local, t_send, t_recv, q_send, q_recv):
     tm, sp = lax.axis_index("tm"), lax.axis_index("space")
     steps, rows, size = f_ref.shape
@@ -159,10 +159,10 @@
 
     sent = []
 
-    def along(source, target, slot, it, distance):
+    def along(source, target, slot, distance):
         copy = pltpu.make_async_remote_copy(
             src_ref=source, dst_ref=target,
-            send_sem=t_send.at[it, slot], recv_sem=t_recv.at[it, slot],
+            send_sem=t_send.at[slot], recv_sem=t_recv.at[slot],
             device_id={"tm": tm + distance}, device_id_type=MESH)
         sent.append((copy, distance))
 
@@ -171,52 +171,84 @@
             copy.start()
         return copy
 
+    last = COARSE_FACTOR - 1
+    shift = along(tbuf.at[last], lrx, 0, 1)
+    drift = gain4 - mid
+    slope = 3.0 * gain4 * mid2 * drift + ratio * (push - top)
+    aref[...] = begin
+
+    @pl.when(tm >= 1)
+    def _():
+        shift.wait_recv()
+        aref[...] = lrx[...]
+
+    arrived = aref[...]
+    ubuf[0] = tbuf[0] + jnp.where(first, gain4 * begin, 0.0)
+    bare = jnp.where(first, 0.0, gain4 * arrived)
+    base = tbuf[0] + gain4 * arrived
+    local = jnp.zeros_like(begin)
+    for i in range(1, last):
+        relaxed = ubuf[0] if i == 1 else tbuf[i - 1]
+        bare = mid * bare + gain4 * relaxed
+        local = mid * local + gain4 * (gain4 * base - bare)
+        base = tbuf[i] + bare
+        ubuf[i] = tbuf[i]
+    ubuf[last] = tbuf[last]
+    rhs = mid * bare + gain4 * tbuf[last - 1]
+    change = gain4 * base - rhs
+    zbuf[0, 0] = rhs
+    zbuf[0, 1] = local + ratio * change
+    near = along(zbuf.at[0], grx.at[0], 1, 1)
+    far = along(zbuf.at[0], grx.at[1], 2, 2)
+    gbuf[...] = change + (1.0 - ratio) * rhs
+    step_in = along(gbuf, wrx, 3, 1)
+    zbuf[1] = jnp.zeros((2,) + begin.shape, F32)
+
+    @pl.when(tm >= 1)
+    def _():
+        near.wait_recv()
+        zbuf[1] = grx[0]
+
+    @pl.when(tm >= 2)
+    def _():
+        far.wait_recv()
+        zbuf[1, 0] = zbuf[1, 0] + top * grx[1, 0]
+        zbuf[1, 1] = zbuf[1, 1] + top * grx[1, 1] + slope * grx[1, 0]
+    slope = 2.0 * top * slope
+    power = top * top
+    for r, d in enumerate(rounds):
+        copy = along(zbuf.at[r + 1], zrx.at[r], 4 + r, d)
+        zbuf[r + 2] = zbuf[r + 1]
+
+        @pl.when(tm >= d)
+        def _():
+            copy.wait_recv()
+            zbuf[r + 2, 0] = zbuf[r + 2, 0] + power * zrx[r, 0]
+            zbuf[r + 2, 1] = zbuf[r + 2, 1] + power * zrx[r, 1] + slope * zrx[r, 0]
+        slope = 2.0 * power * slope
+        power = power * power
+    aref[...] = jnp.zeros_like(begin)
+
+    @pl.when(tm >= 1)
+    def _():
+        step_in.wait_recv()
+        aref[...] = wrx[...] - (1.0 - ratio) * zbuf[len(rounds) + 1, 0]
+
     for it in range(ITERS):
-        last = COARSE_FACTOR - 1
-        newest = gain4 * vref[last] + tbuf[last]
-        lbuf[it] = newest
-        shift = along(lbuf.at[it], lrx.at[it], 0, it, 1)
-        relaxed = [gain4 * vref[i] + tbuf[i] for i in range(last)] + [newest]
-        residual = [None] + [gain4 * (relaxed[i - 1] - vref[i]) for i in range(1, COARSE_FACTOR)]
-        local = residual[1]
-        for i in range(2, COARSE_FACTOR):
-            local = mid * local + residual[i]
-        gbuf[it] = local - jnp.where(first, 0.0, push * vref[0]) + ratio * newest
-        near = along(gbuf.at[it], grx.at[it, 0], 1, it, 1)
-        far = along(gbuf.at[it], grx.at[it, 1], 2, it, 2)
-        for i in range(COARSE_FACTOR):
-            ubuf[i] = relaxed[i]
-        zbuf[it, 0] = jnp.zeros_like(begin)
-        aref[...] = begin
-
-        @pl.when(tm >= 1)
-        def _():
-            shift.wait_recv()
-            aref[...] = lrx[it]
-            near.wait_recv()
-            zbuf[it, 0] = grx[it, 0]
-
-        @pl.when(tm >= 2)
-        def _():
-            far.wait_recv()
-            zbuf[it, 0] = zbuf[it, 0] + top * grx[it, 1]
-        power = top * top
-        for r, d in enumerate(rounds):
-            copy = along(zbuf.at[it, r], zrx.at[it, r], 3 + r, it, d)
-            zbuf[it, r + 1] = zbuf[it, r]
-
-            @pl.when(tm >= d)
-            def _():
-                copy.wait_recv()
-                zbuf[it, r + 1] = zbuf[it, r + 1] + power * zrx[it, r]
-            power = power * power
-        arrived = aref[...]
-        incoming = jnp.where(first, 0.0, zbuf[it, len(rounds)] - ratio * arrived)
         before = vref[0]
+        if it == 0:
+            incoming = zbuf[len(rounds) + 1, 0]
+            ahead = jnp.where(first, 0.0, arrived)
+        else:
+            ahead = aref[...]
+            incoming = zbuf[len(rounds) + 1, 1] - ratio * ahead
+            arrived = before + ahead
+            for i in range(COARSE_FACTOR):
+                ubuf[i] = gain4 * vref[i] + tbuf[i]
         keep = incoming
         for i in range(COARSE_FACTOR):
             if i == 0:
-                res = gain4 * (arrived - before)
+                res = gain4 * ahead
                 run = res
             else:
                 res = gain4 * (ubuf[i - 1] - vref_old)
@@ -347,19 +379,19 @@
             pltpu.VMEM((steps,) + state, F32),
             pltpu.VMEM((COARSE_FACTOR,) + state, F32),
             pltpu.VMEM((COARSE_FACTOR,) + state, F32),
-            pltpu.VMEM((ITERS,) + state, F32),
-            pltpu.VMEM((ITERS,) + state, F32),
-            pltpu.VMEM((ITERS, slots) + state, F32),
-            pltpu.VMEM((ITERS,) + state, F32),
-            pltpu.VMEM((ITERS, 2) + state, F32),
-            pltpu.VMEM((ITERS, slots) + state, F32),
+            pltpu.VMEM(state, F32),
+            pltpu.VMEM((slots + 1, ITERS) + state, F32),
+            pltpu.VMEM(state, F32),
+            pltpu.VMEM(state, F32),
+            pltpu.VMEM((2, ITERS) + state, F32),
+            pltpu.VMEM((slots, ITERS) + state, F32),
             pltpu.VMEM((COARSE_FACTOR + 1,) + state, F32),
             pltpu.VMEM(state, F32),
             pltpu.VMEM((stat_rows, LANES), F32),
             pltpu.VMEM((n_sp, stat_rows, LANES), F32),
             dma((chunks, n_sp)), dma((chunks, n_sp)), dma((chunks,)),
             dma((chunks, n_sp)), dma((chunks, n_sp)), dma((chunks,)),
-            dma((ITERS, 3 + len(rounds))), dma((ITERS, 3 + len(rounds))),
+            dma((4 + len(rounds),)), dma((4 + len(rounds),)),
             dma((n_sp,)), dma((n_sp,)),
         ],
         compiler_params=pltpu.CompilerParams(collective_id=0, has_side_effects=True),

time: 44.6 us -> 45.4 us (1.018)
  Pallas kernels: 40.2 us -> 41 us
    pallas_call x1, Pallas kernels: 40.2 us -> 41 us  [shards(): pl.pallas_call(functools.partial(kernel, n_tm, n_sp, tuple(rounds)), out_...]
where the time goes in v2:
time: 45.4 us; the launch traced here: 45.2 us
  Pallas kernels  41 us (90%)
  local copies, waits for them, and re-layouts  3.52 us (8%)
  between operations  0.65 us (1%)
    pallas_call x1, Pallas kernels, shards(): pl.pallas_call(functools.partial(kernel, n_tm, n_sp, tuple(rounds)), out_...  41 us
    unnamed x7, local copies, waits for them, and re-layouts  3.52 us

profile of v2, /device:TPU:27, one launch (start us, length us, event | category | flops | bytes accessed | tf_op | source)
XLA Modules:
  0.0 45.2 jit_solution(17575588415130901113)
XLA Ops:
  0.6 41.0 %shard_map.85 = (f32[16,64,256]{2,1,0:T(8,128)}, f32[2,4]{1,0:T(2,128)}, f32[2,4]{1,0:T(2,128)}) custom-call(bf16[16,64,256]{2,1,0:T(8,128)(2,1)} %f_ref.1, bf16[64,256]{1,0:T(8,128)(2,1)} %s_ref.1, bf16[256,256]{1,0:T(8,128)(2,1)} %constant.8.clone.half_ref, bf16[256,256]{1,0:T(8,128)(2,1)} %constant.9.clone.low_ref, ...), custom_call_target="tpu_custom_call" | custom-call | tf_op jit(solution)/shard_map/pallas_call | solution.py:366
  41.7 0.0 copy-start.1
  41.7 2.3 %copy.12 = f32[16,64,256]{2,1,0:T(8,128)} copy(f32[16,64,256]{2,1,0:T(8,128)} %get-tuple-element.6) | data formatting | bytes 2097152
  44.0 0.0 copy-done.1
  44.0 0.0 copy-start
  44.0 0.6 %copy.13 = f32[2,4]{1,0:T(2,128)} copy(f32[2,4]{1,0:T(2,128)S(1)} %copy-done.1) | data formatting | bytes 64
  44.5 0.1 copy-done
  44.6 0.6 %copy.14 = f32[2,4]{1,0:T(2,128)} copy(f32[2,4]{1,0:T(2,128)S(1)} %copy-done) | data formatting | bytes 64
Async XLA Ops:
  41.7 2.3 %copy-start.1 = (f32[2,4]{1,0:T(2,128)S(1)}, f32[2,4]{1,0:T(2,128)}, u32[]{:S(2)}) copy-start(f32[2,4]{1,0:T(2,128)} %get-tuple-element.7) | copy-start | bytes 100
  44.0 0.7 %copy-start = (f32[2,4]{1,0:T(2,128)S(1)}, f32[2,4]{1,0:T(2,128)}, u32[]{:S(2)}) copy-start(f32[2,4]{1,0:T(2,128)} %get-tuple-element.8) | copy-start | bytes 100

commit v3 on v2

--- a/solution.py
+++ b/solution.py
@@ -53,8 +53,8 @@
     )
 
 
-def kernel(n_tm, n_sp, rounds, f_ref, s_ref, half_ref, low_ref, back_ref, rate_ref,
-           out_ref, hist_ref, chg_ref,
+def kernel(n_tm, n_sp, rounds, f_ref, s_ref, half_ref, low_ref, rate_ref,
+           out_ref, total_ref,
            sbuf, rbuf, src, path, tbuf, ubuf, gbuf, zbuf, lrx, wrx, grx, zrx, vref, aref, stats, srx,
            f_send, f_recv, f_local, b_send, b_recv, b_local, t_send, t_recv, q_send, q_recv):
     tm, sp = lax.axis_index("tm"), lax.axis_index("space")
@@ -201,7 +201,6 @@
     near = along(zbuf.at[0], grx.at[0], 1, 1)
     far = along(zbuf.at[0], grx.at[1], 2, 2)
     gbuf[...] = change + (1.0 - ratio) * rhs
-    step_in = along(gbuf, wrx, 3, 1)
     zbuf[1] = jnp.zeros((2,) + begin.shape, F32)
 
     @pl.when(tm >= 1)
@@ -216,8 +215,12 @@
         zbuf[1, 1] = zbuf[1, 1] + top * grx[1, 1] + slope * grx[1, 0]
     slope = 2.0 * top * slope
     power = top * top
+    if not rounds:
+        step_in = along(gbuf, wrx, 3, 1)
     for r, d in enumerate(rounds):
         copy = along(zbuf.at[r + 1], zrx.at[r], 4 + r, d)
+        if r == 0:
+            step_in = along(gbuf, wrx, 3, 1)
         zbuf[r + 2] = zbuf[r + 1]
 
         @pl.when(tm >= d)
@@ -309,18 +312,34 @@
         for copy in backward[index][:-1]:
             copy.wait_recv()
         backward[index][-1].wait()
-        block = jnp.concatenate(
-            [rbuf[j, pairs + 1 + lo:pairs + 1 + hi].reshape((hi - lo) * rows, LANES)
-             for j in range(n_sp)], axis=1)
-        heat = jnp.dot(block, back_ref[...], preferred_element_type=F32)
-        out_ref[lo:hi] = heat[:, :size].reshape(hi - lo, rows, size)
-        out_ref[pairs + lo:pairs + hi] = heat[:, size:].reshape(hi - lo, rows, size)
+        out_ref[:, lo:hi] = rbuf[:, pairs + 1 + lo:pairs + 1 + hi]
 
     total = stats[...]
     for k in range(1, n_sp):
         tallies[k - 1].wait_recv()
         total = total + srx[lax.rem(sp - k + n_sp, n_sp)]
-    total = jnp.sum(total, axis=1, keepdims=True)
+    total_ref[...] = total
+
+    for copies in backward:
+        for copy in copies[:-1]:
+            copy.wait_send()
+    for copy in tallies:
+        copy.wait_send()
+    for copy, distance in sent:
+        @pl.when(tm + distance < n_tm)
+        def _():
+            copy.wait_send()
+
+
+def finish(rows_ref, back_ref, total_ref, out_ref, hist_ref, chg_ref):
+    slabs, pairs, rows, _ = rows_ref.shape
+    size = out_ref.shape[-1]
+    block = jnp.concatenate(
+        [rows_ref[j].reshape(pairs * rows, LANES) for j in range(slabs)], axis=1)
+    heat = jnp.dot(block, back_ref[...], preferred_element_type=F32)
+    for part in range(2):
+        out_ref[part] = heat[:, part * size:(part + 1) * size].reshape(pairs, rows, size)
+    total = jnp.sum(total_ref[...], axis=1, keepdims=True)
     points = ITERS * COARSE_FACTOR
     residual_norm = jnp.sqrt(total[:points] / (size * size))
     relative = jnp.sqrt(total[points:2 * points] / total[2 * points:3 * points])
@@ -334,16 +353,6 @@
         chg = jnp.where(where == k, relative[k:k + 1], chg)
     hist_ref[...] = hist
     chg_ref[...] = chg
-
-    for copies in backward:
-        for copy in copies[:-1]:
-            copy.wait_send()
-    for copy in tallies:
-        copy.wait_send()
-    for copy, distance in sent:
-        @pl.when(tm + distance < n_tm)
-        def _():
-            copy.wait_send()
 
 
 def shards(forcing, starting_heat):
@@ -363,15 +372,14 @@
     stat_rows = 3 * ITERS * COARSE_FACTOR
     dma = pltpu.SemaphoreType.DMA
     vmem = pl.BlockSpec(memory_space=pltpu.VMEM)
-    return pl.pallas_call(
+    returned, total = pl.pallas_call(
         functools.partial(kernel, n_tm, n_sp, tuple(rounds)),
         out_shape=(
-            jax.ShapeDtypeStruct((steps, rows, size), F32),
-            jax.ShapeDtypeStruct((ITERS, COARSE_FACTOR), F32),
-            jax.ShapeDtypeStruct((ITERS, COARSE_FACTOR), F32),
+            jax.ShapeDtypeStruct((n_sp, pairs, rows, LANES), BF16),
+            jax.ShapeDtypeStruct((stat_rows, LANES), F32),
         ),
-        in_specs=[vmem] * 6,
-        out_specs=(vmem,) * 3,
+        in_specs=[vmem] * 5,
+        out_specs=(vmem,) * 2,
         scratch_shapes=[
             pltpu.VMEM((n_sp, 2 * pairs + 1, rows, LANES), BF16),
             pltpu.VMEM((n_sp, 2 * pairs + 1, rows, LANES), BF16),
@@ -395,8 +403,24 @@
             dma((n_sp,)), dma((n_sp,)),
         ],
         compiler_params=pltpu.CompilerParams(collective_id=0, has_side_effects=True),
-    )(forcing, starting_heat, jnp.asarray(half), jnp.asarray(low), jnp.asarray(back),
-      jnp.asarray(rate))
+    )(forcing, starting_heat, jnp.asarray(half), jnp.asarray(low), jnp.asarray(rate))
+    small = jax.ShapeDtypeStruct((ITERS, COARSE_FACTOR), F32)
+    heat, history, change = pl.pallas_call(
+        finish,
+        grid=(pairs // 2,),
+        out_shape=(jax.ShapeDtypeStruct((2, pairs, rows, size), F32), small, small),
+        in_specs=[
+            pl.BlockSpec((n_sp, 2, rows, LANES), lambda p: (0, p, 0, 0)),
+            pl.BlockSpec((2 * size, 2 * size), lambda p: (0, 0)),
+            pl.BlockSpec((stat_rows, LANES), lambda p: (0, 0)),
+        ],
+        out_specs=(
+            pl.BlockSpec((2, 2, rows, size), lambda p: (0, p, 0, 0)),
+            pl.BlockSpec(small.shape, lambda p: (0, 0)),
+            pl.BlockSpec(small.shape, lambda p: (0, 0)),
+        ),
+    )(returned, jnp.asarray(back), total)
+    return heat.reshape(steps, rows, size), history, change
 
 
 def solution(mesh):

time: 45.4 us -> 44.2 us (0.974)
  local copies, waits for them, and re-layouts: 3.52 us -> 0 us
  Pallas kernels: 41 us -> 43.3 us
    pallas_call x0 -> x1, Pallas kernels: none -> 3.96 us  [shards(): pl.pallas_call(finish, grid=(pairs // 2,), out_shape=(jax.ShapeDtypeStruc...]
    unnamed x7 -> x0, local copies, waits for them, and re-layouts: 3.52 us -> none
    pallas_call x1, Pallas kernels: 41 us -> 39.4 us  [shards(): pl.pallas_call(functools.partial(kernel, n_tm, n_sp, tuple(rounds)), out_...]
where the time goes in v3:
time: 44.2 us; the launch traced here: 44 us
  Pallas kernels  43.3 us (98%)
  between operations  0.64 us (1%)
    pallas_call x1, Pallas kernels, shards(): pl.pallas_call(functools.partial(kernel, n_tm, n_sp, tuple(rounds)), out_...  39.4 us
    pallas_call x1, Pallas kernels, shards(): pl.pallas_call(finish, grid=(pairs // 2,), out_shape=(jax.ShapeDtypeStruc...  3.96 us

profile of v3, /device:TPU:27, one launch (start us, length us, event | category | flops | bytes accessed | tf_op | source)
XLA Modules:
  0.0 44.0 jit_solution(18229879150820541536)
XLA Ops:
  0.6 39.4 %shard_map.85 = (bf16[4,8,64,128]{3,2,1,0:T(8,128)(2,1)}, f32[24,128]{1,0:T(8,128)}) custom-call(bf16[16,64,256]{2,1,0:T(8,128)(2,1)} %f_ref.1, bf16[64,256]{1,0:T(8,128)(2,1)} %s_ref.1, bf16[256,256]{1,0:T(8,128)(2,1)} %constant.8.clone.half_ref, bf16[256,256]{1,0:T(8,128)(2,1)} %constant.9.clone.low_ref, f32[4,128,128]{2,1,0:T(8,128)} %constant.10.clone.rate_ref), custom_call_target="tpu_custom_call" | custom-call | tf_op jit(solution)/shard_map/pallas_call | solution.py:375
  40.0 4.0 %shard_map.86 = (f32[2,8,64,256]{3,2,1,0:T(8,128)}, f32[2,4]{1,0:T(2,128)}, f32[2,4]{1,0:T(2,128)}) custom-call(bf16[4,8,64,128]{3,2,1,0:T(8,128)(2,1)} %get-tuple-element.8.rows_ref, bf16[512,512]{1,0:T(8,128)(2,1)} %constant.11.clone.back_ref, f32[24,128]{1,0:T(8,128)} %get-tuple-element.9.total_ref), custom_call_target="tpu_custom_call" | custom-call | tf_op jit(solution)/shard_map/pallas_call | solution.py:408

commit v4 on v1

--- a/solution.py
+++ b/solution.py
@@ -53,8 +53,8 @@
     )
 
 
-def kernel(n_tm, n_sp, rounds, f_ref, s_ref, half_ref, low_ref, back_ref, rate_ref,
-           out_ref, hist_ref, chg_ref,
+def kernel(n_tm, n_sp, rounds, f_ref, s_ref, half_ref, low_ref, rate_ref,
+           out_ref, total_ref,
            sbuf, rbuf, src, path, tbuf, ubuf, lbuf, gbuf, zbuf, lrx, grx, zrx, vref, aref, stats, srx,
            f_send, f_recv, f_local, b_send, b_recv, b_local, t_send, t_recv, q_send, q_recv):
     tm, sp = lax.axis_index("tm"), lax.axis_index("space")
@@ -277,18 +277,34 @@
         for copy in backward[index][:-1]:
             copy.wait_recv()
         backward[index][-1].wait()
-        block = jnp.concatenate(
-            [rbuf[j, pairs + 1 + lo:pairs + 1 + hi].reshape((hi - lo) * rows, LANES)
-             for j in range(n_sp)], axis=1)
-        heat = jnp.dot(block, back_ref[...], preferred_element_type=F32)
-        out_ref[lo:hi] = heat[:, :size].reshape(hi - lo, rows, size)
-        out_ref[pairs + lo:pairs + hi] = heat[:, size:].reshape(hi - lo, rows, size)
+        out_ref[:, lo:hi] = rbuf[:, pairs + 1 + lo:pairs + 1 + hi]
 
     total = stats[...]
     for k in range(1, n_sp):
         tallies[k - 1].wait_recv()
         total = total + srx[lax.rem(sp - k + n_sp, n_sp)]
-    total = jnp.sum(total, axis=1, keepdims=True)
+    total_ref[...] = total
+
+    for copies in backward:
+        for copy in copies[:-1]:
+            copy.wait_send()
+    for copy in tallies:
+        copy.wait_send()
+    for copy, distance in sent:
+        @pl.when(tm + distance < n_tm)
+        def _():
+            copy.wait_send()
+
+
+def finish(rows_ref, back_ref, total_ref, out_ref, hist_ref, chg_ref):
+    slabs, pairs, rows, _ = rows_ref.shape
+    size = out_ref.shape[-1]
+    block = jnp.concatenate(
+        [rows_ref[j].reshape(pairs * rows, LANES) for j in range(slabs)], axis=1)
+    heat = jnp.dot(block, back_ref[...], preferred_element_type=F32)
+    for part in range(2):
+        out_ref[part] = heat[:, part * size:(part + 1) * size].reshape(pairs, rows, size)
+    total = jnp.sum(total_ref[...], axis=1, keepdims=True)
     points = ITERS * COARSE_FACTOR
     residual_norm = jnp.sqrt(total[:points] / (size * size))
     relative = jnp.sqrt(total[points:2 * points] / total[2 * points:3 * points])
@@ -302,16 +318,6 @@
         chg = jnp.where(where == k, relative[k:k + 1], chg)
     hist_ref[...] = hist
     chg_ref[...] = chg
-
-    for copies in backward:
-        for copy in copies[:-1]:
-            copy.wait_send()
-    for copy in tallies:
-        copy.wait_send()
-    for copy, distance in sent:
-        @pl.when(tm + distance < n_tm)
-        def _():
-            copy.wait_send()
 
 
 def shards(forcing, starting_heat):
@@ -331,15 +337,14 @@
     stat_rows = 3 * ITERS * COARSE_FACTOR
     dma = pltpu.SemaphoreType.DMA
     vmem = pl.BlockSpec(memory_space=pltpu.VMEM)
-    return pl.pallas_call(
+    returned, total = pl.pallas_call(
         functools.partial(kernel, n_tm, n_sp, tuple(rounds)),
         out_shape=(
-            jax.ShapeDtypeStruct((steps, rows, size), F32),
-            jax.ShapeDtypeStruct((ITERS, COARSE_FACTOR), F32),
-            jax.ShapeDtypeStruct((ITERS, COARSE_FACTOR), F32),
+            jax.ShapeDtypeStruct((n_sp, pairs, rows, LANES), BF16),
+            jax.ShapeDtypeStruct((stat_rows, LANES), F32),
         ),
-        in_specs=[vmem] * 6,
-        out_specs=(vmem,) * 3,
+        in_specs=[vmem] * 5,
+        out_specs=(vmem,) * 2,
         scratch_shapes=[
             pltpu.VMEM((n_sp, 2 * pairs + 1, rows, LANES), BF16),
             pltpu.VMEM((n_sp, 2 * pairs + 1, rows, LANES), BF16),
@@ -363,8 +368,24 @@
             dma((n_sp,)), dma((n_sp,)),
         ],
         compiler_params=pltpu.CompilerParams(collective_id=0, has_side_effects=True),
-    )(forcing, starting_heat, jnp.asarray(half), jnp.asarray(low), jnp.asarray(back),
-      jnp.asarray(rate))
+    )(forcing, starting_heat, jnp.asarray(half), jnp.asarray(low), jnp.asarray(rate))
+    small = jax.ShapeDtypeStruct((ITERS, COARSE_FACTOR), F32)
+    heat, history, change = pl.pallas_call(
+        finish,
+        grid=(pairs // 2,),
+        out_shape=(jax.ShapeDtypeStruct((2, pairs, rows, size), F32), small, small),
+        in_specs=[
+            pl.BlockSpec((n_sp, 2, rows, LANES), lambda p: (0, p, 0, 0)),
+            pl.BlockSpec((2 * size, 2 * size), lambda p: (0, 0)),
+            pl.BlockSpec((stat_rows, LANES), lambda p: (0, 0)),
+        ],
+        out_specs=(
+            pl.BlockSpec((2, 2, rows, size), lambda p: (0, p, 0, 0)),
+            pl.BlockSpec(small.shape, lambda p: (0, 0)),
+            pl.BlockSpec(small.shape, lambda p: (0, 0)),
+        ),
+    )(returned, jnp.asarray(back), total)
+    return heat.reshape(steps, rows, size), history, change
 
 
 def solution(mesh):

time: 44.6 us -> 44.3 us (level)
  local copies, waits for them, and re-layouts: 3.52 us -> 0 us
  Pallas kernels: 40.2 us -> 43.5 us
    pallas_call x0 -> x1, Pallas kernels: none -> 3.96 us  [shards(): pl.pallas_call(finish, grid=(pairs // 2,), out_shape=(jax.ShapeDtypeStruc...]
    unnamed x7 -> x0, local copies, waits for them, and re-layouts: 3.52 us -> none
    pallas_call x1, Pallas kernels: 40.2 us -> 39.5 us  [shards(): pl.pallas_call(functools.partial(kernel, n_tm, n_sp, tuple(rounds)), out_...]
where the time goes in v4:
time: 44.3 us; the launch traced here: 44.1 us
  Pallas kernels  43.5 us (98%)
  between operations  0.64 us (1%)
    pallas_call x1, Pallas kernels, shards(): pl.pallas_call(functools.partial(kernel, n_tm, n_sp, tuple(rounds)), out_...  39.5 us
    pallas_call x1, Pallas kernels, shards(): pl.pallas_call(finish, grid=(pairs // 2,), out_shape=(jax.ShapeDtypeStruc...  3.96 us

profile of v4, /device:TPU:27, one launch (start us, length us, event | category | flops | bytes accessed | tf_op | source)
XLA Modules:
  0.0 44.1 jit_solution(4648270667434014113)
XLA Ops:
  0.6 39.5 %shard_map.85 = (bf16[4,8,64,128]{3,2,1,0:T(8,128)(2,1)}, f32[24,128]{1,0:T(8,128)}) custom-call(bf16[16,64,256]{2,1,0:T(8,128)(2,1)} %f_ref.1, bf16[64,256]{1,0:T(8,128)(2,1)} %s_ref.1, bf16[256,256]{1,0:T(8,128)(2,1)} %constant.8.clone.half_ref, bf16[256,256]{1,0:T(8,128)(2,1)} %constant.9.clone.low_ref, f32[4,128,128]{2,1,0:T(8,128)} %constant.10.clone.rate_ref), custom_call_target="tpu_custom_call" | custom-call | tf_op jit(solution)/shard_map/pallas_call | solution.py:340
  40.2 4.0 %shard_map.86 = (f32[2,8,64,256]{3,2,1,0:T(8,128)}, f32[2,4]{1,0:T(2,128)}, f32[2,4]{1,0:T(2,128)}) custom-call(bf16[4,8,64,128]{3,2,1,0:T(8,128)(2,1)} %get-tuple-element.8.rows_ref, bf16[512,512]{1,0:T(8,128)(2,1)} %constant.11.clone.back_ref, f32[24,128]{1,0:T(8,128)} %get-tuple-element.9.total_ref), custom_call_target="tpu_custom_call" | custom-call | tf_op jit(solution)/shard_map/pallas_call | solution.py:373
